TPU v7x, 32 devices: a whole 2x2x4 slice. The times are simulated.
32 devices in a mesh: pix: 8 (over z, y), rep: 4 (over x, core).
Axes of the slice: x: 2, y: 2, z: 4, core: 2. Of those that a mesh axis runs over, the one named last changes fastest.
Arguments:
- interferograms: float32 [256, 131072], P(('pix', 'rep')), may hold values from -6 to 6
- epoch_pairs: int32 [2, 256], replicated, may hold values from 0 to 63, as said below
- los: float32 [3, 131072], P(None, ('pix', 'rep')), may hold values from 0.3 to 1
- patch_place: int32 [2, 4096], replicated, may hold values from 0 to 255, as said below
- patch_depth: int32 [4096], replicated, may hold values from 0 to 7
Outputs:
- predicted: float32 [64, 131072], P(None, ('pix', 'rep'))
- slip: float32 [64, 4096], P(None, ('pix', 'rep'))
Inputs may be any that keep to these rules, and one draw needn't show every extreme that they name: `epoch_pairs`: row 0 holds an interferogram's earlier epoch and row 1 its later one; the two always differ. `patch_place`: row 0 is an east cell below 256; row 1 is a north cell below 32.
All inputs are finite; a program needn't handle non-finite values.
Results may differ from a plain program's by a relative error of at most 0.0037.
Values may be sent and summed in bfloat16 or wider, within the bound.
A program may use at most 64 MiB of HBM per device.

v0:
```python
import jax
import jax.numpy as jnp
from jax import lax
from jax.sharding import PartitionSpec as P

NEP = 64
IMG_W = 1024
pixel_step = 0.1
patch_step = 0.4
damping = 0.5
depth_base = 0.5
depth_step = 0.25


def sbas_inverse(epoch_pairs, epochs_count):
    epochs = lax.iota(jnp.int32, epochs_count)
    design = (epochs[None, :] == epoch_pairs[1][:, None]).astype(jnp.float32) - (
        epochs[None, :] == epoch_pairs[0][:, None]
    ).astype(jnp.float32)
    normal = jnp.dot(design.T, design, precision=lax.Precision.HIGHEST) + damping * jnp.eye(
        epochs_count, dtype=jnp.float32
    )
    factor = jnp.linalg.cholesky(normal)
    return jax.scipy.linalg.cho_solve((factor, True), design.T)


def green_tile(pixel, los_rows, patch_place, patch_depth):
    column = (pixel % IMG_W).astype(jnp.float32)
    line = (pixel // IMG_W).astype(jnp.float32)
    xpos = (column + 0.5) * pixel_step
    ypos = (line + 0.5) * pixel_step
    patch_x = (patch_place[0].astype(jnp.float32) + 0.5) * patch_step
    patch_y = (patch_place[1].astype(jnp.float32) + 0.5) * patch_step
    patch_z = depth_base + depth_step * patch_depth.astype(jnp.float32)
    delta_x = xpos[:, None] - patch_x[None, :]
    delta_y = ypos[:, None] - patch_y[None, :]
    delta_z = patch_z[None, :]
    dist_sq = delta_x * delta_x + delta_y * delta_y + delta_z * delta_z
    toward = (
        los_rows[0][:, None] * delta_x
        + los_rows[1][:, None] * delta_y
        + los_rows[2][:, None] * delta_z
    )
    return (delta_z * toward / (dist_sq * jnp.sqrt(dist_sq))).astype(jnp.bfloat16)


def on_device(interferograms, epoch_pairs, los, patch_place, patch_depth):
    devices = lax.axis_size(("pix", "rep"))
    ifg_dev, total = interferograms.shape
    pix_dev = total // devices
    epochs_count = NEP
    npatch = patch_depth.shape[0]
    own = npatch // devices
    pseudo = sbas_inverse(epoch_pairs, epochs_count)
    pieces = interferograms.reshape(ifg_dev, devices, pix_dev)
    series = jnp.dot(
        pseudo,
        lax.all_to_all(pieces, ("pix", "rep"), split_axis=1, concat_axis=0, tiled=True)[:, 0, :],
        precision=lax.Precision.HIGHEST,
        preferred_element_type=jnp.float32,
    )
    anchor = lax.axis_index(("pix", "rep")) * pix_dev
    width = min(512, pix_dev)
    count = pix_dev // width

    def tile_at(index):
        start = index * width
        pixel = anchor + start + lax.iota(jnp.int32, width)
        los_rows = lax.dynamic_slice_in_dim(los, start, width, 1)
        return (green_tile(pixel, los_rows, patch_place, patch_depth), start)

    def first_step(index, carry):
        rhs, bound = carry
        tile, start = tile_at(index)
        resid = lax.dynamic_slice_in_dim(series, start, width, 1).astype(jnp.bfloat16)
        rhs = rhs + jnp.dot(resid, tile, preferred_element_type=jnp.float32)
        magnitude = jnp.abs(tile)
        weight = jnp.sum(magnitude.astype(jnp.float32), axis=1).astype(jnp.bfloat16)
        bound = bound + jnp.dot(weight[None, :], magnitude, preferred_element_type=jnp.float32)
        return (rhs, bound)

    zero_rhs = jnp.zeros((epochs_count, npatch), jnp.float32)
    zero_bound = jnp.zeros((1, npatch), jnp.float32)
    rhs, bound = lax.fori_loop(0, count, first_step, (zero_rhs, zero_bound))
    rhs_all, bound_all = lax.psum((rhs, bound), ("pix", "rep"))
    slip_all = rhs_all / bound_all
    sweep_slip_half = slip_all.astype(jnp.bfloat16)

    def sweep_step(index, rhs_now):
        tile, start = tile_at(index)
        guess = lax.dot_general(
            sweep_slip_half, tile, (((1,), (1,)), ((), ())), preferred_element_type=jnp.float32
        )
        resid = (lax.dynamic_slice_in_dim(series, start, width, 1) - guess).astype(jnp.bfloat16)
        return rhs_now + jnp.dot(resid, tile, preferred_element_type=jnp.float32)

    rhs = lax.fori_loop(0, count, sweep_step, zero_rhs)
    slip_all = slip_all + lax.psum(rhs, ("pix", "rep")) / bound_all
    slip_half = slip_all.astype(jnp.bfloat16)
    slip_own = lax.dynamic_slice_in_dim(slip_all, lax.axis_index(("pix", "rep")) * own, own, 1)

    def final_step(index, predicted):
        tile, start = tile_at(index)
        block = lax.dot_general(
            slip_half, tile, (((1,), (1,)), ((), ())), preferred_element_type=jnp.float32
        )
        return lax.dynamic_update_slice_in_dim(predicted, block, start, 1)

    predicted = lax.fori_loop(0, count, final_step, jnp.zeros((epochs_count, pix_dev), jnp.float32))
    return (predicted, slip_own)


def solution(mesh):
    placed = (P(("pix", "rep"), None), P(), P(None, ("pix", "rep")), P(), P())
    return jax.shard_map(
        on_device,
        mesh=mesh,
        in_specs=placed,
        out_specs=(P(None, ("pix", "rep")), P(None, ("pix", "rep"))),
        check_vma=False,
    )
```

profile of v0, /device:TPU:0, one launch (start us, length us, event | category | flops | bytes accessed | tf_op | source)
XLA Modules:
  0.0 731.8 jit_solution(1607313868562399574)
XLA Ops:
  7.2 7.5 %all-to-all-start = ((f32[8,32,4096]{2,0,1:T(8,128)}), f32[8,32,4096]{2,0,1:T(8,128)}, u32[]{:S(2)}, u32[]{:S(2)}) async-start(f32[8,32,4096]{2,0,1:T(8,128)} %bitcast.110), calls=%async_computation | async-start | bytes 8388608 | tf_op jit(solution)/shard_map/all_to_all | solution.py:58
  28.2 80.2 %all-to-all-done = f32[8,32,4096]{2,0,1:T(8,128)} async-done(((f32[8,32,4096]{2,0,1:T(8,128)}), f32[8,32,4096]{2,0,1:T(8,128)}, u32[]{:S(2)}, u32[]{:S(2)}) %all-to-all-start) | async-done | bytes 4194336 | tf_op jit(solution)/shard_map/all_to_all | solution.py:58
  114.1 168.4 %while.53 = (s32[]{:T(128)}, f32[64,4096]{1,0:T(8,128)S(1)}, f32[1,4096]{1,0:T(1,128)S(1)}, bf16[64,4096]{1,0:T(8,128)(2,1)S(1)}, f32[1,4096]{1,0:T(1,128)S(1)},...) while((s32[]{:T(128)}, f32[64,4096]{1,0:T(8,128)S(1)}, ...), condition=%wide.region_4.5_spmd.clone, body=%wide.region_2.4_spmd.clone.sunk | while | flops 373867008 | bytes 2590974 | solution.py:84
  115.3 6.6 convolution_add_fusion.6
  121.9 6.8 abs_reduce_fusion.2
  136.3 6.6 convolution_add_fusion.6
  142.8 6.8 abs_reduce_fusion.2
  157.3 6.6 convolution_add_fusion.6
  163.8 6.8 abs_reduce_fusion.2
  178.2 6.6 convolution_add_fusion.6
  184.8 6.8 abs_reduce_fusion.2
  199.2 6.6 convolution_add_fusion.6
  205.8 6.8 abs_reduce_fusion.2
  220.2 6.6 convolution_add_fusion.6
  226.8 6.8 abs_reduce_fusion.2
  241.2 6.6 convolution_add_fusion.6
  247.7 6.8 abs_reduce_fusion.2
  262.1 6.6 convolution_add_fusion.6
  268.7 6.8 abs_reduce_fusion.2
  283.6 38.4 %psum.22 = f32[4096]{0:T(1024)S(1)} all-reduce(f32[4096]{0:T(1024)S(1)} %bitcast.147), channel_id=1, replica_groups=mesh['pix'=8,'rep'=4] {'pix','rep'}, use_global_device_ids=true, to_apply=%region_6.7 | all-reduce | flops 4096 | bytes 32768 | tf_op jit(solution)/shard_map/psum | solution.py:85
  322.0 92.1 %all-reduce.3.cloned.1.call-done = f32[64,4096]{1,0:T(8,128)} async-done(((f32[64,4096]{1,0:T(8,128)}), f32[64,4096]{1,0:T(8,128)}) %all-reduce.3.cloned.1.call-update) | async-done | bytes 1048592 | tf_op jit(solution)/shard_map/psum | solution.py:85
  415.4 117.2 %while.54 = (s32[]{:T(128)}, f32[64,4096]{1,0:T(8,128)S(1)}, f32[64,4096]{1,0:T(8,128)}, f32[1,4096]{1,0:T(1,128)S(1)}, f32[3,4096]{1,0:T(4,128)}, /*index=5*/s3...) while((s32[]{:T(128)}, f32[64,4096]{1,0:T(8,128)S(1)}, ...), condition=%wide.region_8.9_spmd.clone, body=%wide.region_7.8_spmd.clone.sunk | while | flops 600417280 | bytes 3068157 | solution.py:97
  416.4 13.6 %convolution_add_fusion.8 = f32[64,4096]{1,0:T(8,128)S(1)} fusion(f32[4096]{0:T(1024)S(1)} %mul.1511, f32[512]{0:T(512)S(1)} %bitcast.143, f32[4096]{0:T(1024)S(1)} %bitcast.128, f32[512]{0:T(512)S(1)} %get-tuple-element.1055, f32[512]{0:T(512)S(1)} %bitcast.142, f32[4096]{0:T(1024)S(1)} %bitcast.129, f32[512]{0:T(512)S(1)} %get-tuple-element.1058, ...), kind=kOutput, calls=%fused_computation.86.clone.1 | convolution fusion | flops 600375296 | bytes 2904069 | tf_op jit(solution)/shard_map/while/body/eval_jaxpr/dot_general | solution.py:95
  431.0 13.6 %convolution_add_fusion.8 = f32[64,4096]{1,0:T(8,128)S(1)} fusion(f32[4096]{0:T(1024)S(1)} %mul.1511, f32[512]{0:T(512)S(1)} %bitcast.143, f32[4096]{0:T(1024)S(1)} %bitcast.128, f32[512]{0:T(512)S(1)} %get-tuple-element.1055, f32[512]{0:T(512)S(1)} %bitcast.142, f32[4096]{0:T(1024)S(1)} %bitcast.129, f32[512]{0:T(512)S(1)} %get-tuple-element.1058, ...), kind=kOutput, calls=%fused_computation.86.clone.1 | convolution fusion | flops 600375296 | bytes 2904069 | tf_op jit(solution)/shard_map/while/body/eval_jaxpr/dot_general | solution.py:95
  445.6 13.6 %convolution_add_fusion.8 = f32[64,4096]{1,0:T(8,128)S(1)} fusion(f32[4096]{0:T(1024)S(1)} %mul.1511, f32[512]{0:T(512)S(1)} %bitcast.143, f32[4096]{0:T(1024)S(1)} %bitcast.128, f32[512]{0:T(512)S(1)} %get-tuple-element.1055, f32[512]{0:T(512)S(1)} %bitcast.142, f32[4096]{0:T(1024)S(1)} %bitcast.129, f32[512]{0:T(512)S(1)} %get-tuple-element.1058, ...), kind=kOutput, calls=%fused_computation.86.clone.1 | convolution fusion | flops 600375296 | bytes 2904069 | tf_op jit(solution)/shard_map/while/body/eval_jaxpr/dot_general | solution.py:95
  460.3 13.6 %convolution_add_fusion.8 = f32[64,4096]{1,0:T(8,128)S(1)} fusion(f32[4096]{0:T(1024)S(1)} %mul.1511, f32[512]{0:T(512)S(1)} %bitcast.143, f32[4096]{0:T(1024)S(1)} %bitcast.128, f32[512]{0:T(512)S(1)} %get-tuple-element.1055, f32[512]{0:T(512)S(1)} %bitcast.142, f32[4096]{0:T(1024)S(1)} %bitcast.129, f32[512]{0:T(512)S(1)} %get-tuple-element.1058, ...), kind=kOutput, calls=%fused_computation.86.clone.1 | convolution fusion | flops 600375296 | bytes 2904069 | tf_op jit(solution)/shard_map/while/body/eval_jaxpr/dot_general | solution.py:95
  474.9 13.6 %convolution_add_fusion.8 = f32[64,4096]{1,0:T(8,128)S(1)} fusion(f32[4096]{0:T(1024)S(1)} %mul.1511, f32[512]{0:T(512)S(1)} %bitcast.143, f32[4096]{0:T(1024)S(1)} %bitcast.128, f32[512]{0:T(512)S(1)} %get-tuple-element.1055, f32[512]{0:T(512)S(1)} %bitcast.142, f32[4096]{0:T(1024)S(1)} %bitcast.129, f32[512]{0:T(512)S(1)} %get-tuple-element.1058, ...), kind=kOutput, calls=%fused_computation.86.clone.1 | convolution fusion | flops 600375296 | bytes 2904069 | tf_op jit(solution)/shard_map/while/body/eval_jaxpr/dot_general | solution.py:95
  489.5 13.6 %convolution_add_fusion.8 = f32[64,4096]{1,0:T(8,128)S(1)} fusion(f32[4096]{0:T(1024)S(1)} %mul.1511, f32[512]{0:T(512)S(1)} %bitcast.143, f32[4096]{0:T(1024)S(1)} %bitcast.128, f32[512]{0:T(512)S(1)} %get-tuple-element.1055, f32[512]{0:T(512)S(1)} %bitcast.142, f32[4096]{0:T(1024)S(1)} %bitcast.129, f32[512]{0:T(512)S(1)} %get-tuple-element.1058, ...), kind=kOutput, calls=%fused_computation.86.clone.1 | convolution fusion | flops 600375296 | bytes 2904069 | tf_op jit(solution)/shard_map/while/body/eval_jaxpr/dot_general | solution.py:95
  504.1 13.6 %convolution_add_fusion.8 = f32[64,4096]{1,0:T(8,128)S(1)} fusion(f32[4096]{0:T(1024)S(1)} %mul.1511, f32[512]{0:T(512)S(1)} %bitcast.143, f32[4096]{0:T(1024)S(1)} %bitcast.128, f32[512]{0:T(512)S(1)} %get-tuple-element.1055, f32[512]{0:T(512)S(1)} %bitcast.142, f32[4096]{0:T(1024)S(1)} %bitcast.129, f32[512]{0:T(512)S(1)} %get-tuple-element.1058, ...), kind=kOutput, calls=%fused_computation.86.clone.1 | convolution fusion | flops 600375296 | bytes 2904069 | tf_op jit(solution)/shard_map/while/body/eval_jaxpr/dot_general | solution.py:95
  518.8 13.6 %convolution_add_fusion.8 = f32[64,4096]{1,0:T(8,128)S(1)} fusion(f32[4096]{0:T(1024)S(1)} %mul.1511, f32[512]{0:T(512)S(1)} %bitcast.143, f32[4096]{0:T(1024)S(1)} %bitcast.128, f32[512]{0:T(512)S(1)} %get-tuple-element.1055, f32[512]{0:T(512)S(1)} %bitcast.142, f32[4096]{0:T(1024)S(1)} %bitcast.129, f32[512]{0:T(512)S(1)} %get-tuple-element.1058, ...), kind=kOutput, calls=%fused_computation.86.clone.1 | convolution fusion | flops 600375296 | bytes 2904069 | tf_op jit(solution)/shard_map/while/body/eval_jaxpr/dot_general | solution.py:95
  533.5 129.8 %all-reduce.5.cloned.1.call-done = f32[64,4096]{1,0:T(8,128)} async-done(((f32[64,4096]{1,0:T(8,128)}), f32[64,4096]{1,0:T(8,128)}) %all-reduce.5.cloned.1.call-update) | async-done | bytes 1048592 | tf_op jit(solution)/shard_map/psum | solution.py:98
  664.8 59.0 %while.52 = (s32[]{:T(128)}, f32[64,4096]{1,0:T(8,128)S(1)}, f32[1,4096]{1,0:T(1,128)S(1)}, f32[3,4096]{1,0:T(4,128)}, s32[]{:T(128)}, /*index=5*/f32[1,4096]{1,...) while((s32[]{:T(128)}, f32[64,4096]{1,0:T(8,128)S(1)}, ...), condition=%wide.region_11.12_spmd, body=%wide.region_10.11_spmd.sunk | while | flops 299934720 | bytes 895211 | solution.py:109
  (185 shorter events, 151.6 us)
Async XLA Ops:
  7.2 7.6 %copy-start.7 = (s32[2,256]{1,0:T(2,128)S(1)}, s32[2,256]{1,0:T(2,128)}, u32[]{:S(2)}) copy-start(s32[2,256]{1,0:T(2,128)} %param.12) | copy-start | bytes 6148
  7.2 20.3 %copy-start.6 = (s32[4096]{0:T(1024)S(1)}, s32[4096]{0:T(1024)}, u32[]{:S(2)}) copy-start(s32[4096]{0:T(1024)} %param.15) | copy-start | bytes 49156
  7.2 20.9 %copy-start.5 = (s32[2,4096]{1,0:T(2,128)S(1)}, s32[2,4096]{1,0:T(2,128)}, u32[]{:S(2)}) copy-start(s32[2,4096]{1,0:T(2,128)} %param.14) | copy-start | bytes 98308
  7.2 101.2 %all-to-all-start = ((f32[8,32,4096]{2,0,1:T(8,128)}), f32[8,32,4096]{2,0,1:T(8,128)}, u32[]{:S(2)}, u32[]{:S(2)}) async-start(f32[8,32,4096]{2,0,1:T(8,128)} %bitcast.110), calls=%async_computation | async-start | bytes 8388608 | tf_op jit(solution)/shard_map/all_to_all | solution.py:58
  14.7 399.4 %all-reduce.3.cloned.1.call-start = ((), (), s32[]{:S(2)}) async-start(), calls=%async_computation.1 | async-start | bytes 2097152 | tf_op jit(solution)/shard_map/psum | solution.py:85
  282.5 1.0 copy-start.1
  283.5 379.8 %all-reduce.5.cloned.1.call-start = ((), (), s32[]{:S(2)}) async-start(), calls=%async_computation.2 | async-start | bytes 2097152 | tf_op jit(solution)/shard_map/psum | solution.py:98
  322.0 93.4 %copy-start.4 = (f32[4096]{0:T(1024)}, f32[4096]{0:T(1024)S(1)}, u32[]{:S(2)}) copy-start(f32[4096]{0:T(1024)S(1)} %psum.22) | copy-start | bytes 49156
  415.4 248.0 %copy-start = (f32[64,4096]{1,0:T(8,128)S(1)}, f32[64,4096]{1,0:T(8,128)}, u32[]{:S(2)}) copy-start(f32[64,4096]{1,0:T(8,128)} %all-reduce.3.cloned.1.call-done) | copy-start | bytes 3145732
  532.5 1.0 copy-start.2
  723.8 1.0 copy-start.3
Sparse Core Ops, SparseCore 0:
  283.7 130.3 all-reduce.2
  533.7 129.6 all-reduce.4
where the time goes:
time: 738 us; the launch traced here: 732 us
  waiting for transfers between devices  302 us (41%)
  matrix products  271 us (37%)
  other arithmetic  71.6 us (10%)
  blocking collectives  38.4 us (5%)
  local copies, waits for them, and re-layouts  24.6 us (3%)
  between operations  14.5 us (2%)
  starting transfers between devices  7.54 us (1%)
    psum x1, waiting for transfers between devices, on_device(): slip_all = slip_all + lax.psum(rhs, ('pix', 'rep')) / bound_all  130 us
    dot_general x8, matrix products, sweep_step(): return rhs_now + jnp.dot(resid, tile, preferred_element_type=jnp.float32)  109 us
    psum x1, waiting for transfers between devices, on_device(): rhs_all, bound_all = lax.psum((rhs, bound), ('pix', 'rep'))  92.1 us
    all_to_all x1, waiting for transfers between devices, on_device(): lax.all_to_all(pieces, ('pix', 'rep'), split_axis=1, concat_axis=0, tiled...  80.2 us
    reduce_sum x8, other arithmetic, first_step(): weight = jnp.sum(magnitude.astype(jnp.float32), axis=1).astype(jnp.bfloat16)  54.8 us
    dot_general x8, matrix products, first_step(): rhs = rhs + jnp.dot(resid, tile, preferred_element_type=jnp.float32)  52.5 us
    dot_general x8, matrix products, first_step(): jnp.dot(weight[None, :], magnitude, preferred_element_type=jnp.float32)  52.4 us
    dot_general x8, matrix products, final_step(): lax.dot_general(slip_half, tile, (((1,), (1,)), ((), ())), preferred_elem...  50.8 us
  transfers between devices with their start and end apart: 3, of which 3 were waited for; matrix products, arithmetic and copies ran while one was open for 2% of the time, Pallas kernels for 0%

commit v1 on v0

--- a/solution.py
+++ b/solution.py
@@ -95,7 +95,7 @@
         return rhs_now + jnp.dot(resid, tile, preferred_element_type=jnp.float32)
 
     rhs = lax.fori_loop(0, count, sweep_step, zero_rhs)
-    slip_all = slip_all + lax.psum(rhs, ("pix", "rep")) / bound_all
+    slip_all = slip_all + jnp.sum(lax.all_gather(rhs, ("pix", "rep")), axis=0) / bound_all
     slip_half = slip_all.astype(jnp.bfloat16)
     slip_own = lax.dynamic_slice_in_dim(slip_all, lax.axis_index(("pix", "rep")) * own, own, 1)
 

time: 738 us -> 821 us (1.11)
  waiting for transfers between devices: 302 us -> 366 us
  other arithmetic: 71.6 us -> 83 us
  matrix products: 271 us -> 280 us
    all_gather x0 -> x1, waiting for transfers between devices: none -> 193 us  [on_device(): lax.all_gather(rhs, ('pix', 'rep'))]
    psum x1 -> x0, waiting for transfers between devices: 130 us -> none  [on_device(): slip_all = slip_all + lax.psum(rhs, ('pix', 'rep')) / bound_all]
    reduce_sum x0 -> x1, other arithmetic: none -> 11.9 us  [on_device(): jnp.sum(lax.all_gather(rhs, ('pix', 'rep')), axis=0) / bound_all]
    dot_general x8, matrix products: 50.8 us -> 59.1 us  [final_step(): lax.dot_general(slip_half, tile, (((1,), (1,)), ((), ())), preferred_elem...]
where the time goes in v1:
time: 821 us; the launch traced here: 815 us
  waiting for transfers between devices  366 us (45%)
  matrix products  280 us (34%)
  other arithmetic  83 us (10%)
  blocking collectives  38.4 us (5%)
  local copies, waits for them, and re-layouts  24.6 us (3%)
  between operations  14.5 us (2%)
    all_gather x1, waiting for transfers between devices, on_device(): lax.all_gather(rhs, ('pix', 'rep'))  193 us
    dot_general x8, matrix products, sweep_step(): return rhs_now + jnp.dot(resid, tile, preferred_element_type=jnp.float32)  109 us
    psum x1, waiting for transfers between devices, on_device(): rhs_all, bound_all = lax.psum((rhs, bound), ('pix', 'rep'))  92.1 us
    all_to_all x1, waiting for transfers between devices, on_device(): lax.all_to_all(pieces, ('pix', 'rep'), split_axis=1, concat_axis=0, tiled...  80.2 us
    dot_general x8, matrix products, final_step(): lax.dot_general(slip_half, tile, (((1,), (1,)), ((), ())), preferred_elem...  59.1 us
    reduce_sum x8, other arithmetic, first_step(): weight = jnp.sum(magnitude.astype(jnp.float32), axis=1).astype(jnp.bfloat16)  54.8 us
    dot_general x8, matrix products, first_step(): rhs = rhs + jnp.dot(resid, tile, preferred_element_type=jnp.float32)  52.5 us
    dot_general x8, matrix products, first_step(): jnp.dot(weight[None, :], magnitude, preferred_element_type=jnp.float32)  52.4 us
  transfers between devices with their start and end apart: 3, of which 3 were waited for; matrix products, arithmetic and copies ran while one was open for 2% of the time, Pallas kernels for 0%

profile of v1, /device:TPU:0, one launch (start us, length us, event | category | flops | bytes accessed | tf_op | source)
XLA Modules:
  0.0 815.1 jit_solution(7307088277148498381)
XLA Ops:
  7.2 7.5 all-to-all-start
  28.2 80.2 %all-to-all-done = f32[8,32,4096]{2,0,1:T(8,128)} async-done(((f32[8,32,4096]{2,0,1:T(8,128)}), f32[8,32,4096]{2,0,1:T(8,128)}, u32[]{:S(2)}, u32[]{:S(2)}) %all-to-all-start) | async-done | bytes 4194336 | tf_op jit(solution)/shard_map/all_to_all | solution.py:58
  114.1 168.4 %while.53 = (s32[]{:T(128)}, f32[64,4096]{1,0:T(8,128)S(1)}, f32[1,4096]{1,0:T(1,128)S(1)}, bf16[64,4096]{1,0:T(8,128)(2,1)S(1)}, f32[1,4096]{1,0:T(1,128)S(1)},...) while((s32[]{:T(128)}, f32[64,4096]{1,0:T(8,128)S(1)}, ...), condition=%wide.region_4.5_spmd.clone, body=%wide.region_2.4_spmd.clone.sunk | while | flops 373867008 | bytes 2590974 | solution.py:84
  121.9 6.8 abs_reduce_fusion.2
  142.8 6.8 abs_reduce_fusion.2
  163.8 6.8 abs_reduce_fusion.2
  184.8 6.8 abs_reduce_fusion.2
  205.8 6.8 abs_reduce_fusion.2
  226.8 6.8 abs_reduce_fusion.2
  268.7 6.8 abs_reduce_fusion.2
  283.6 38.4 %psum.15 = f32[4096]{0:T(1024)S(1)} all-reduce(f32[4096]{0:T(1024)S(1)} %bitcast.149), channel_id=1, replica_groups=mesh['pix'=8,'rep'=4] {'pix','rep'}, use_global_device_ids=true, to_apply=%region_6.7 | all-reduce | flops 4096 | bytes 32768 | tf_op jit(solution)/shard_map/psum | solution.py:85
  322.0 92.1 %all-reduce.2.cloned.1.call-done = f32[64,4096]{1,0:T(8,128)} async-done(((f32[64,4096]{1,0:T(8,128)}), f32[64,4096]{1,0:T(8,128)}) %all-reduce.2.cloned.1.call-update) | async-done | bytes 1048592 | tf_op jit(solution)/shard_map/psum | solution.py:85
  415.4 117.2 %while.54 = (s32[]{:T(128)}, f32[64,4096]{1,0:T(8,128)S(1)}, f32[64,4096]{1,0:T(8,128)}, f32[1,4096]{1,0:T(1,128)S(1)}, f32[3,4096]{1,0:T(4,128)}, /*index=5*/s3...) while((s32[]{:T(128)}, f32[64,4096]{1,0:T(8,128)S(1)}, ...), condition=%wide.region_8.9_spmd.clone, body=%wide.region_7.8_spmd.clone.sunk | while | flops 600417280 | bytes 3068157 | solution.py:97
  416.4 13.6 %convolution_add_fusion.8 = f32[64,4096]{1,0:T(8,128)S(1)} fusion(f32[4096]{0:T(1024)S(1)} %mul.1511, f32[512]{0:T(512)S(1)} %bitcast.145, f32[4096]{0:T(1024)S(1)} %bitcast.130, f32[512]{0:T(512)S(1)} %get-tuple-element.1055, f32[512]{0:T(512)S(1)} %bitcast.144, f32[4096]{0:T(1024)S(1)} %bitcast.131, f32[512]{0:T(512)S(1)} %get-tuple-element.1058, ...), kind=kOutput, calls=%fused_computation.86.clone.1 | convolution fusion | flops 600375296 | bytes 2904069 | tf_op jit(solution)/shard_map/while/body/eval_jaxpr/dot_general | solution.py:95
  431.0 13.6 %convolution_add_fusion.8 = f32[64,4096]{1,0:T(8,128)S(1)} fusion(f32[4096]{0:T(1024)S(1)} %mul.1511, f32[512]{0:T(512)S(1)} %bitcast.145, f32[4096]{0:T(1024)S(1)} %bitcast.130, f32[512]{0:T(512)S(1)} %get-tuple-element.1055, f32[512]{0:T(512)S(1)} %bitcast.144, f32[4096]{0:T(1024)S(1)} %bitcast.131, f32[512]{0:T(512)S(1)} %get-tuple-element.1058, ...), kind=kOutput, calls=%fused_computation.86.clone.1 | convolution fusion | flops 600375296 | bytes 2904069 | tf_op jit(solution)/shard_map/while/body/eval_jaxpr/dot_general | solution.py:95
  445.7 13.6 %convolution_add_fusion.8 = f32[64,4096]{1,0:T(8,128)S(1)} fusion(f32[4096]{0:T(1024)S(1)} %mul.1511, f32[512]{0:T(512)S(1)} %bitcast.145, f32[4096]{0:T(1024)S(1)} %bitcast.130, f32[512]{0:T(512)S(1)} %get-tuple-element.1055, f32[512]{0:T(512)S(1)} %bitcast.144, f32[4096]{0:T(1024)S(1)} %bitcast.131, f32[512]{0:T(512)S(1)} %get-tuple-element.1058, ...), kind=kOutput, calls=%fused_computation.86.clone.1 | convolution fusion | flops 600375296 | bytes 2904069 | tf_op jit(solution)/shard_map/while/body/eval_jaxpr/dot_general | solution.py:95
  460.3 13.6 %convolution_add_fusion.8 = f32[64,4096]{1,0:T(8,128)S(1)} fusion(f32[4096]{0:T(1024)S(1)} %mul.1511, f32[512]{0:T(512)S(1)} %bitcast.145, f32[4096]{0:T(1024)S(1)} %bitcast.130, f32[512]{0:T(512)S(1)} %get-tuple-element.1055, f32[512]{0:T(512)S(1)} %bitcast.144, f32[4096]{0:T(1024)S(1)} %bitcast.131, f32[512]{0:T(512)S(1)} %get-tuple-element.1058, ...), kind=kOutput, calls=%fused_computation.86.clone.1 | convolution fusion | flops 600375296 | bytes 2904069 | tf_op jit(solution)/shard_map/while/body/eval_jaxpr/dot_general | solution.py:95
  474.9 13.6 %convolution_add_fusion.8 = f32[64,4096]{1,0:T(8,128)S(1)} fusion(f32[4096]{0:T(1024)S(1)} %mul.1511, f32[512]{0:T(512)S(1)} %bitcast.145, f32[4096]{0:T(1024)S(1)} %bitcast.130, f32[512]{0:T(512)S(1)} %get-tuple-element.1055, f32[512]{0:T(512)S(1)} %bitcast.144, f32[4096]{0:T(1024)S(1)} %bitcast.131, f32[512]{0:T(512)S(1)} %get-tuple-element.1058, ...), kind=kOutput, calls=%fused_computation.86.clone.1 | convolution fusion | flops 600375296 | bytes 2904069 | tf_op jit(solution)/shard_map/while/body/eval_jaxpr/dot_general | solution.py:95
  489.5 13.6 %convolution_add_fusion.8 = f32[64,4096]{1,0:T(8,128)S(1)} fusion(f32[4096]{0:T(1024)S(1)} %mul.1511, f32[512]{0:T(512)S(1)} %bitcast.145, f32[4096]{0:T(1024)S(1)} %bitcast.130, f32[512]{0:T(512)S(1)} %get-tuple-element.1055, f32[512]{0:T(512)S(1)} %bitcast.144, f32[4096]{0:T(1024)S(1)} %bitcast.131, f32[512]{0:T(512)S(1)} %get-tuple-element.1058, ...), kind=kOutput, calls=%fused_computation.86.clone.1 | convolution fusion | flops 600375296 | bytes 2904069 | tf_op jit(solution)/shard_map/while/body/eval_jaxpr/dot_general | solution.py:95
  504.2 13.6 %convolution_add_fusion.8 = f32[64,4096]{1,0:T(8,128)S(1)} fusion(f32[4096]{0:T(1024)S(1)} %mul.1511, f32[512]{0:T(512)S(1)} %bitcast.145, f32[4096]{0:T(1024)S(1)} %bitcast.130, f32[512]{0:T(512)S(1)} %get-tuple-element.1055, f32[512]{0:T(512)S(1)} %bitcast.144, f32[4096]{0:T(1024)S(1)} %bitcast.131, f32[512]{0:T(512)S(1)} %get-tuple-element.1058, ...), kind=kOutput, calls=%fused_computation.86.clone.1 | convolution fusion | flops 600375296 | bytes 2904069 | tf_op jit(solution)/shard_map/while/body/eval_jaxpr/dot_general | solution.py:95
  518.8 13.6 %convolution_add_fusion.8 = f32[64,4096]{1,0:T(8,128)S(1)} fusion(f32[4096]{0:T(1024)S(1)} %mul.1511, f32[512]{0:T(512)S(1)} %bitcast.145, f32[4096]{0:T(1024)S(1)} %bitcast.130, f32[512]{0:T(512)S(1)} %get-tuple-element.1055, f32[512]{0:T(512)S(1)} %bitcast.144, f32[4096]{0:T(1024)S(1)} %bitcast.131, f32[512]{0:T(512)S(1)} %get-tuple-element.1058, ...), kind=kOutput, calls=%fused_computation.86.clone.1 | convolution fusion | flops 600375296 | bytes 2904069 | tf_op jit(solution)/shard_map/while/body/eval_jaxpr/dot_general | solution.py:95
  533.6 193.3 %all-gather.3.cloned.1.call-done = f32[2048,4096]{1,0:T(8,128)} async-done(((f32[64,4096]{1,0:T(8,128)}), f32[2048,4096]{1,0:T(8,128)}) %all-gather.3.cloned.1.call-update) | async-done | bytes 33554448 | tf_op jit(solution)/shard_map/all_gather | solution.py:98
  726.8 11.9 %reduce_sum.23 = f32[64,4096]{1,0:T(8,128)S(1)} reduce(f32[32,64,4096]{2,1,0:T(8,128)} %bitcast.110, f32[]{:T(128)} %constant.489.clone.1), dimensions={0}, to_apply=%region_9.10 | reduce | flops 8126464 | bytes 34603012 | tf_op jit(solution)/shard_map/reduce_sum | solution.py:98
  739.8 67.3 %while.52 = (s32[]{:T(128)}, f32[64,4096]{1,0:T(8,128)S(1)}, f32[1,4096]{1,0:T(1,128)S(1)}, f32[3,4096]{1,0:T(4,128)}, s32[]{:T(128)}, /*index=5*/f32[1,4096]{1,...) while((s32[]{:T(128)}, f32[64,4096]{1,0:T(8,128)S(1)}, ...), condition=%wide.region_11.12_spmd, body=%wide.region_10.11_spmd.sunk | while | flops 299934720 | bytes 895211 | solution.py:109
  740.8 7.4 fusion.114
  749.2 7.4 fusion.114
  757.6 7.4 fusion.114
  766.0 7.4 fusion.114
  774.4 7.4 fusion.114
  782.9 7.4 fusion.114
  791.3 7.4 fusion.114
  799.7 7.4 fusion.114
  (188 shorter events, 159.7 us)
Async XLA Ops:
  7.2 7.6 copy-start.8
  7.2 20.3 %copy-start.7 = (s32[4096]{0:T(1024)S(1)}, s32[4096]{0:T(1024)}, u32[]{:S(2)}) copy-start(s32[4096]{0:T(1024)} %param.15) | copy-start | bytes 49156
  7.2 20.9 %copy-start.6 = (s32[2,4096]{1,0:T(2,128)S(1)}, s32[2,4096]{1,0:T(2,128)}, u32[]{:S(2)}) copy-start(s32[2,4096]{1,0:T(2,128)} %param.14) | copy-start | bytes 98308
  7.2 101.2 %all-to-all-start = ((f32[8,32,4096]{2,0,1:T(8,128)}), f32[8,32,4096]{2,0,1:T(8,128)}, u32[]{:S(2)}, u32[]{:S(2)}) async-start(f32[8,32,4096]{2,0,1:T(8,128)} %bitcast.112), calls=%async_computation | async-start | bytes 8388608 | tf_op jit(solution)/shard_map/all_to_all | solution.py:58
  14.7 399.4 %all-reduce.2.cloned.1.call-start = ((), (), s32[]{:S(2)}) async-start(), calls=%async_computation.1 | async-start | bytes 2097152 | tf_op jit(solution)/shard_map/psum | solution.py:85
  282.5 1.0 copy-start.1
  283.5 443.3 %all-gather.3.cloned.1.call-start = ((), (), s32[]{:S(2)}) async-start(), calls=%async_computation.2 | async-start | bytes 34603008 | tf_op jit(solution)/shard_map/all_gather | solution.py:98
  321.9 93.4 %copy-start.4 = (f32[4096]{0:T(1024)}, f32[4096]{0:T(1024)S(1)}, u32[]{:S(2)}) copy-start(f32[4096]{0:T(1024)S(1)} %psum.15) | copy-start | bytes 49156
  532.6 1.0 copy-start.2
  726.8 11.9 %copy-start = (f32[64,4096]{1,0:T(8,128)S(1)}, f32[64,4096]{1,0:T(8,128)}, u32[]{:S(2)}) copy-start(f32[64,4096]{1,0:T(8,128)} %all-reduce.2.cloned.1.call-done) | copy-start | bytes 3145732
  726.8 11.9 %copy-start.5 = (f32[4096]{0:T(1024)S(1)}, f32[4096]{0:T(1024)}, u32[]{:S(2)}) copy-start(f32[4096]{0:T(1024)} %copy-done.4) | copy-start | bytes 49156
  807.1 1.0 copy-start.3
Sparse Core Ops, SparseCore 0:
  283.6 130.3 all-reduce.1
  533.7 193.1 all-gather.2
